TPU v7x, 64 devices: a 2x2x8 block of a 4x4x8 slice. The times are simulated.
64 devices in a mesh: dp: 4 (over x, y), sp: 16 (over z, core).
Axes of the slice: x: 2, y: 2, z: 8, core: 2. Of those that a mesh axis runs over, the one named last changes fastest.
The devices are a block of a 4x4x8 slice.
Arguments:
- patches: bfloat16 [64, 8192, 512], P('dp', 'sp'), parts along dimension 0
- ln1_scale: float32 [512], replicated
- ln1_bias: float32 [512], replicated
- w_tok1: bfloat16 [8192, 256], replicated
- b_tok1: float32 [256], replicated
- w_tok2: bfloat16 [256, 8192], replicated
- b_tok2: float32 [8192], replicated
- ln2_scale: float32 [512], replicated
- ln2_bias: float32 [512], replicated
- w_ch1: bfloat16 [512, 2048], replicated
- b_ch1: float32 [2048], replicated
- w_ch2: bfloat16 [2048, 512], replicated
- b_ch2: float32 [512], replicated
Outputs:
- output: bfloat16 [64, 8192, 512], P('dp', 'sp'), parts along dimension 0
There are 4 independent parts. A program takes and returns all parts, laid end to end along the dimension named above; an argument that names none is the same for every part.
All inputs are finite; a program needn't handle non-finite values.
Results may differ from a plain program's by a relative error of at most 0.0111177.
Values are sent between devices in bfloat16 or wider.
A program may use at most 768 MiB of HBM per device.

v0:
```python
import jax
import jax.numpy as jnp
from jax import lax
from jax.sharding import PartitionSpec as P

LN_EPS = 1e-6


def layer_norm(rows, scale, offset):
    rows_wide = rows.astype(jnp.float32)
    row_mean = jnp.mean(rows_wide, axis=-1, keepdims=True)
    centered = rows_wide - row_mean
    row_var = jnp.mean(centered * centered, axis=-1, keepdims=True)
    return (centered * lax.rsqrt(row_var + LN_EPS) * scale + offset).astype(jnp.bfloat16)


def channel_mixing(residual, ln2_scale, ln2_bias, w_ch1, b_ch1, w_ch2, b_ch2):
    chan_in = layer_norm(residual, ln2_scale, ln2_bias)
    pre_act = jnp.einsum('bsc,ce->bse', chan_in, w_ch1, preferred_element_type=jnp.float32) + b_ch1
    act_ch = jax.nn.gelu(pre_act, approximate=True).astype(jnp.bfloat16)
    ch_out = jnp.einsum('bse,ec->bsc', act_ch, w_ch2, preferred_element_type=jnp.float32) + b_ch2
    return (residual.astype(jnp.float32) + ch_out).astype(jnp.bfloat16)


def solution(mesh):
    row_spec = P('dp', 'sp', None)
    full_spec = P()

    def local_layer(patches, ln1_scale, ln1_bias, w_tok1, b_tok1, w_tok2, b_tok2, ln2_scale, ln2_bias, w_ch1, b_ch1, w_ch2, b_ch2):
        normed = layer_norm(patches, ln1_scale, ln1_bias)
        normed_cols = lax.all_to_all(normed, 'sp', 2, 1, tiled=True)
        hidden = jnp.einsum('sd,bsc->bdc', w_tok1, normed_cols, preferred_element_type=jnp.float32)
        act_tok = jax.nn.gelu(hidden + b_tok1[None, :, None], approximate=True).astype(jnp.bfloat16)
        mixed = jnp.einsum('ds,bdc->bsc', w_tok2, act_tok, preferred_element_type=jnp.float32)
        mixed_cols = (mixed + b_tok2[None, :, None]).astype(jnp.bfloat16)
        mixed_rows = lax.all_to_all(mixed_cols, 'sp', 1, 2, tiled=True)
        residual = (patches.astype(jnp.float32) + mixed_rows.astype(jnp.float32)).astype(jnp.bfloat16)
        return channel_mixing(residual, ln2_scale, ln2_bias, w_ch1, b_ch1, w_ch2, b_ch2)

    return jax.shard_map(local_layer, mesh=mesh, in_specs=(row_spec,) + (full_spec,) * 12, out_specs=row_spec, check_vma=False)
```

profile of v0, /device:TPU:21, one launch (start us, length us, event | category | flops | bytes accessed | tf_op | source)
XLA Modules:
  0.0 713.3 jit_solution(15518772582492631968)
XLA Ops:
  0.0 4.7 convert_reduce_fusion.1
  4.8 0.0 slice-start.1
  4.8 6.0 fusion.18
  10.8 5.2 fusion.21
  16.0 14.9 %copy.32 = bf16[16,512,512]{1,0,2:T(8,128)(2,1)} copy(bf16[16,512,512]{2,1,0:T(8,128)(2,1)} %fusion.21) | data formatting | bytes 16777216 | tf_op jit(solution)/shard_map/convert_element_type | solution.py:14
  30.9 196.1 %all_to_all.27 = bf16[16,512,512]{1,0,2:T(8,128)(2,1)} all-to-all(bf16[16,512,512]{1,0,2:T(8,128)(2,1)} %copy.32), channel_id=1, replica_groups=mesh['dp'=4,'sp'=16] {'sp'}, dimensions={2} | all-to-all | bytes 16777216 | tf_op jit(solution)/shard_map/all_to_all | solution.py:31
  227.0 11.5 %copy.34 = bf16[16,16,512,32]{2,1,3,0:T(8,128)(2,1)} copy(bf16[16,16,512,32]{2,0,3,1:T(8,128)(2,1)} %bitcast.61) | data formatting | bytes 16777216 | tf_op jit(solution)/shard_map/all_to_all | solution.py:31
  238.5 13.5 %all_to_all.23 = bf16[16,8192,32]{1,2,0:T(8,128)(2,1)} reshape(bf16[16,16,512,32]{2,1,3,0:T(8,128)(2,1)} %copy.34) | data formatting | bytes 16777216 | tf_op jit(solution)/shard_map/all_to_all | solution.py:31
  252.0 7.1 fusion.62
  259.2 5.8 fusion.24
  264.9 34.6 %copy.35 = bf16[16,8192,32]{2,0,1:T(8,128)(2,1)} copy(bf16[16,8192,32]{1,2,0:T(8,128)(2,1)} %fusion.24) | data formatting | bytes 16777216 | tf_op jit(solution)/shard_map/convert_element_type | solution.py:35
  299.5 35.0 %reshape.42 = bf16[16,2,131072]{2,1,0:T(2,128)(2,1)} reshape(bf16[8192,16,32]{2,1,0:T(8,128)(2,1)} %bitcast.54) | data formatting | bytes 16777216
  334.5 189.9 %all_to_all.28 = bf16[16,2,131072]{2,1,0:T(2,128)(2,1)} all-to-all(bf16[16,2,131072]{2,1,0:T(2,128)(2,1)} %reshape.42), channel_id=1, replica_groups=mesh['dp'=4,'sp'=16] {'sp'}, dimensions={0} | all-to-all | bytes 16777216 | tf_op jit(solution)/shard_map/all_to_all | solution.py:36
  524.4 22.8 %reshape.43 = bf16[8192,16,32]{2,1,0:T(8,128)(2,1)} reshape(bf16[16,2,131072]{2,1,0:T(2,128)(2,1)} %all_to_all.28) | data formatting | bytes 16777216
  547.3 33.7 %copy.36 = bf16[16,8192,32]{1,2,0:T(8,128)(2,1)} copy(bf16[16,8192,32]{2,0,1:T(8,128)(2,1)} %bitcast.55) | data formatting | bytes 16777216 | tf_op jit(solution)/shard_map/all_to_all | solution.py:36
  581.0 11.3 %convert_element_type.60 = f32[16,8192,32]{1,2,0:T(8,128)} convert(bf16[16,8192,32]{1,2,0:T(8,128)(2,1)} %copy.36) | non-fusion elementwise | flops 4194304 | bytes 25165824 | tf_op jit(solution)/shard_map/convert_element_type | solution.py:37
  592.3 18.6 %copy.40 = f32[64,8,16,512]{3,2,1,0:T(8,128)S(1)} copy(f32[64,8,16,512]{3,1,2,0:T(8,128)} %bitcast.58) | data formatting | bytes 33554432
  610.9 11.7 %copy.37 = f32[16,512,16,32]{1,3,2,0:T(8,128)} copy(f32[16,512,16,32]{1,2,3,0:T(8,128)S(1)} %bitcast.59) | data formatting | bytes 33554432 | tf_op jit(solution)/shard_map/convert_element_type | solution.py:37
  622.6 17.6 %copy.38 = f32[16,512,512]{2,1,0:T(8,128)} copy(f32[16,512,512]{1,2,0:T(8,128)} %bitcast.60) | data formatting | bytes 33554432 | tf_op jit(solution)/shard_map/convert_element_type | solution.py:37
  640.2 9.1 %convert_reduce_fusion = (f32[16,512]{1,0:T(8,128)S(1)}, bf16[16,512,512]{2,1,0:T(8,128)(2,1)S(1)}) fusion(f32[16,512,512]{2,1,0:T(8,128)} %copy.38, bf16[16,512,512]{2,1,0:T(8,128)(2,1)} %param.13), kind=kLoop, calls=%fused_computation.12 | loop fusion | flops 20963328 | bytes 33587200 | tf_op jit(solution)/shard_map/reduce_sum | solution.py:11
  649.3 3.5 fusion.14
  652.9 0.0 copy-start.9
  652.9 34.0 %fusion.81 = bf16[16,512,2048]{2,1,0:T(8,128)(2,1)} fusion(f32[2048]{0:T(1024)S(1)} %copy-done.6, bf16[16,512,512]{2,1,0:T(8,128)(2,1)S(1)} %get-tuple-element.6, f32[512]{0:T(512)S(1)} %copy-done.7, f32[512]{0:T(512)S(1)} %copy-done.8, f32[16,512]{1,0:T(8,128)S(1)} %add_rsqrt_fusion, f32[16,512]{1,0:T(8,128)S(1)} %broadcast_multiply_fusion, ...), kind=kOutput, calls=%fused_computation.8.clone.clone.clone.clone.1 | convolution fusion | flops 17372807168 | bytes 44118016 | tf_op jit(solution)/shard_map/bsc,ce->bse/dot_general | solution.py:19
  687.0 25.9 %fusion.23 = bf16[16,512,512]{2,1,0:T(8,128)(2,1)} fusion(bf16[16,512,512]{2,1,0:T(8,128)(2,1)S(1)} %get-tuple-element.6, f32[512]{0:T(512)S(1)} %copy-done.9, bf16[2048,512]{1,0:T(8,128)(2,1)} %param.24, bf16[16,512,2048]{2,1,0:T(8,128)(2,1)} %fusion.81), kind=kOutput, calls=%fused_computation.29 | convolution fusion | flops 17196646400 | bytes 52430848 | tf_op jit(solution)/shard_map/bse,ec->bsc/dot_general | solution.py:21
  (29 shorter events, 0.1 us)
Async XLA Ops:
  0.0 652.9 %copy-start = (bf16[512,2048]{1,0:T(8,128)(2,1)S(1)}, bf16[512,2048]{1,0:T(8,128)(2,1)}, u32[]{:S(2)}) copy-start(bf16[512,2048]{1,0:T(8,128)(2,1)} %param.22) | copy-start | bytes 6291460
  0.0 10.8 %slice-start = ((s8[8388608]{0:T(1024)(128)(4,1)}), s8[4194304]{0:T(1024)(128)(4,1)S(1)}, s32[]{:S(2)}) async-start(s8[8388608]{0:T(1024)(128)(4,1)} %bitcast.56), calls=%async_computation.2 | async-start | bytes 8388608
  0.0 10.8 %copy-start.2 = (f32[512]{0:T(512)S(1)}, f32[512]{0:T(512)}, u32[]{:S(2)}) copy-start(f32[512]{0:T(512)} %param.15) | copy-start | bytes 6148
  0.0 10.8 %copy-start.3 = (f32[512]{0:T(512)S(1)}, f32[512]{0:T(512)}, u32[]{:S(2)}) copy-start(f32[512]{0:T(512)} %param.14) | copy-start | bytes 6148
  4.8 6.1 slice-start.1
  227.0 25.0 %copy-start.10 = (f32[256]{0:T(256)S(1)}, f32[256]{0:T(256)}, u32[]{:S(2)}) copy-start(f32[256]{0:T(256)} %param.17) | copy-start | bytes 3076
  238.5 20.6 %copy-start.5 = (f32[8192]{0:T(1024)S(1)}, f32[8192]{0:T(1024)}, u32[]{:S(2)}) copy-start(f32[8192]{0:T(1024)} %param.19) | copy-start | bytes 98308
  252.0 7.1 %copy-start.4 = (bf16[256,8192]{1,0:T(8,128)(2,1)S(1)}, bf16[256,8192]{1,0:T(8,128)(2,1)}, u32[]{:S(2)}) copy-start(bf16[256,8192]{1,0:T(8,128)(2,1)} %param.18) | copy-start | bytes 12582916
  640.2 12.7 %copy-start.6 = (f32[2048]{0:T(1024)S(1)}, f32[2048]{0:T(1024)}, u32[]{:S(2)}) copy-start(f32[2048]{0:T(1024)} %param.23) | copy-start | bytes 24580
  640.2 12.7 %copy-start.7 = (f32[512]{0:T(512)S(1)}, f32[512]{0:T(512)}, u32[]{:S(2)}) copy-start(f32[512]{0:T(512)} %param.21) | copy-start | bytes 6148
  640.2 12.7 %copy-start.8 = (f32[512]{0:T(512)S(1)}, f32[512]{0:T(512)}, u32[]{:S(2)}) copy-start(f32[512]{0:T(512)} %param.20) | copy-start | bytes 6148
  652.9 34.1 %copy-start.9 = (f32[512]{0:T(512)S(1)}, f32[512]{0:T(512)}, u32[]{:S(2)}) copy-start(f32[512]{0:T(512)} %param.25) | copy-start | bytes 6148
  687.0 25.9 %copy-start.1 = (bf16[512,2048]{1,0:T(8,128)(2,1)S(1)}, bf16[512,2048]{1,0:T(8,128)(2,1)}, u32[]{:S(2)}) copy-start(bf16[512,2048]{1,0:T(8,128)(2,1)} %param.22) | copy-start | bytes 6291460
where the time goes:
time: 720 us; the launch traced here: 713 us
  blocking collectives  386 us (54%)
  local copies, waits for them, and re-layouts  214 us (30%)
  matrix products  72.8 us (10%)
  other arithmetic  39.8 us (6%)
    all_to_all x1, blocking collectives, local_layer(): normed_cols = lax.all_to_all(normed, 'sp', 2, 1, tiled=True)  196 us
    all_to_all x1, blocking collectives, local_layer(): mixed_rows = lax.all_to_all(mixed_cols, 'sp', 1, 2, tiled=True)  190 us
    unnamed x29, local copies, waits for them, and re-layouts  76.5 us
    convert_element_type x1, local copies, waits for them, and re-layouts, local_layer(): mixed_cols = (mixed + b_tok2[None, :, None]).astype(jnp.bfloat16)  34.6 us
    dot_general x1, matrix products, channel_mixing(): jnp.einsum('bsc,ce->bse', chan_in, w_ch1, preferred_element_type=jnp.floa...  34 us
    all_to_all x1, local copies, waits for them, and re-layouts, local_layer(): mixed_rows = lax.all_to_all(mixed_cols, 'sp', 1, 2, tiled=True)  33.7 us
    convert_element_type x2, local copies, waits for them, and re-layouts, local_layer(): mixed_rows.astype(jnp.float32)  29.3 us
    dot_general x1, matrix products, channel_mixing(): jnp.einsum('bse,ec->bsc', act_ch, w_ch2, preferred_element_type=jnp.float32)  25.9 us

commit v1 on v0

v1 whole, which is shorter than its diff:
```python
import functools

import jax
import jax.numpy as jnp
from jax import lax
from jax.experimental import pallas as pl
from jax.experimental.pallas import tpu as pltpu
from jax.sharding import PartitionSpec as P

LN_EPS = 1e-6
GELU_K = 0.7978845608028654
F32 = jnp.float32
BF16 = jnp.bfloat16
VMEM_LIMIT = 67043328


def layer_norm(wide, scale, offset):
    mean = jnp.mean(wide, axis=-1, keepdims=True)
    centered = wide - mean
    var = jnp.mean(centered * centered, axis=-1, keepdims=True)
    return (centered * lax.rsqrt(var + LN_EPS) * scale + offset).astype(BF16)


def gelu_of_half(half):
    inner = half * (half * half * (8.0 * 0.044715 * GELU_K) + 2.0 * GELU_K)
    return half + half * jnp.tanh(inner)


def lanes(col, width):
    return jnp.concatenate([col] * (width // 128), axis=1)


def column(row):
    return jnp.broadcast_to(row, (128, row.shape[1])).T


def norm_and_project(x_img, ln1s, ln1b, wt1t, u_s, h_img):
    seq, ch = u_s.shape
    step = 128
    for r in range(0, seq, step):
        u_s[r:r + step, :] = layer_norm(x_img[r:r + step, :].astype(F32), ln1s[...], ln1b[...])
    h_img[...] = jnp.dot(wt1t[...], u_s[...], preferred_element_type=F32)


def token_out_and_channel_mix(x_img, g_img, wt2t, bcol2, ln2s, ln2b, w1, b1h, w2, b2, x1_s, v_s, q_s, o_img, rows=256, wide=512):
    seq, ch = v_s.shape
    hid = w1.shape[1]
    for r in range(0, seq, rows):
        rs = slice(r, r + rows)
        mixed = jnp.dot(wt2t[rs, :], g_img[...], preferred_element_type=F32)
        mixed = (mixed + lanes(bcol2[rs, :], ch)).astype(BF16)
        x1 = (x_img[rs, :].astype(F32) + mixed.astype(F32)).astype(BF16)
        x1_s[rs, :] = x1
        v_s[rs, :] = layer_norm(x1.astype(F32), ln2s[...], ln2b[...])
        for e in range(0, hid, wide):
            es = slice(e, e + wide)
            half = jnp.dot(v_s[rs, :], w1[:, es], preferred_element_type=F32) + b1h[:, es]
            q_s[rs, es] = gelu_of_half(half).astype(BF16)
        y = jnp.dot(q_s[rs, :], w2[...], preferred_element_type=F32) + b2[...]
        o_img[rs, :] = (x1_s[rs, :].astype(F32) + y).astype(BF16)


def fused_kernel(nz, x_hbm, ln1s, ln1b, wt1_hbm, bt1, wt2_hbm, bt2, ln2s, ln2b, w1_hbm, b1, w2_hbm, b2, out_hbm,
                 x_v, h_v, d2d_v, rs_v, g_v, wt1_v, wt1t, wt2_v, wt2t, bcol1, bcol2, w1, w2, b1h, u_s, x1_s, v_s, q_s, o_v,
                 x_sem, w_sem, o_sem, send_sem, dr_sem, rr_sem, ar_sem, gr_sem):
    units, seq, ch = x_v.shape
    tok_hid = h_v.shape[1]
    hid = w1.shape[1]
    half_rows = tok_hid // 2
    piece = half_rows // nz
    hop = nz // 2
    me = lax.axis_index('sp')
    z = lax.div(me, 2)
    c = lax.rem(me, 2)
    right = lax.rem(z + 1, nz) * 2 + c
    left = lax.rem(z + nz - 1, nz) * 2 + c
    mate = z * 2 + (1 - c)
    side = (right, left)

    def at_z(offset):
        return lax.rem(z + nz + offset, nz)

    barrier = pltpu.get_barrier_semaphore()
    for peer in (mate, right, left):
        pl.semaphore_signal(barrier, inc=1, device_id={'sp': peer}, device_id_type=pl.DeviceIdType.MESH)

    def load_x(u):
        return pltpu.make_async_copy(x_hbm.at[u], x_v.at[u], x_sem.at[u])

    first = pl.multiple_of(me * seq, seq)
    loads = [
        pltpu.make_async_copy(wt1_hbm.at[pl.ds(first, seq), :], wt1_v, w_sem.at[0]),
        pltpu.make_async_copy(wt2_hbm.at[:, pl.ds(first, seq)], wt2_v, w_sem.at[1]),
        pltpu.make_async_copy(w1_hbm, w1, w_sem.at[2]),
        pltpu.make_async_copy(w2_hbm, w2, w_sem.at[3]),
    ]
    loads[0].start()
    for u in range(units):
        load_x(u).start()
    for load in loads[1:]:
        load.start()

    def remote(src, dst, slot, u, recv, peer):
        return pltpu.make_async_remote_copy(
            src_ref=src, dst_ref=dst, send_sem=send_sem.at[slot, lax.rem(u, 2)], recv_sem=recv,
            device_id={'sp': peer}, device_id_type=pl.DeviceIdType.MESH)

    def pair_copy(u):
        rows = pl.ds(pl.multiple_of((1 - c) * half_rows, half_rows), half_rows)
        return remote(h_v.at[u, rows, :], d2d_v.at[u], 0, u, dr_sem.at[u], mate)

    def piece_rows(home, lo, n):
        return pl.ds(pl.multiple_of(c * half_rows + home * piece + lo, 8), n)

    def sum_part(way, k):
        if k > 1:
            return 0, piece
        return (0 if way == 0 else piece // 2), piece // 2

    def sum_home(way, k):
        return at_z(hop + 1 - k) if way == 0 else at_z(-(hop + 1 - k))

    def sum_copy(u, way, k):
        lo, n = sum_part(way, k)
        return remote(h_v.at[u, piece_rows(sum_home(way, k), lo, n), :], rs_v.at[u, way, k - 1, pl.ds(lo, n), :],
                      1 + way * hop + k - 1, u, rr_sem.at[u, way, k - 1], side[way])

    def gather_cols(way, k):
        if k < hop:
            return pl.ds(0, ch)
        return pl.ds(0 if way == 0 else ch // 2, ch // 2)

    def gather_copy(u, way, k, shift):
        d = k - 1 + shift
        home = at_z(-d) if way == 0 else at_z(d)
        rows = pl.ds(pl.multiple_of(c * half_rows + home * piece, piece), piece)
        ref = g_v.at[u, rows, gather_cols(way, k)]
        return remote(ref, ref, 1 + 2 * hop + way * hop + k - 1, u, ar_sem.at[u, way, k - 1], side[way])

    def share_copy(u, core):
        rows = pl.ds(pl.multiple_of(core * half_rows, half_rows), half_rows)
        ref = g_v.at[u, rows, :]
        return remote(ref, ref, 1 + 4 * hop, u, gr_sem.at[u], mate)

    def launch(u, copy):
        @pl.when(u >= 2)
        def _():
            copy.wait_send()
        copy.start()

    def project(u):
        load_x(u).wait()
        norm_and_project(x_v.at[u], ln1s, ln1b, wt1t, u_s, h_v.at[u])

    def own_rows():
        return pl.ds(pl.multiple_of(c * half_rows, half_rows), half_rows)

    def add_stage(u, s):
        if s == 1:
            pair_copy(u).wait_recv()
            h_v[u, own_rows(), :] = h_v[u, own_rows(), :] + d2d_v[u]
        elif s <= hop:
            for way in range(2):
                k = s - 1
                sum_copy(u, way, k).wait_recv()
                lo, n = sum_part(way, k)
                rows = piece_rows(sum_home(way, s), lo, n)
                h_v[u, rows, :] = h_v[u, rows, :] + rs_v[u, way, k - 1, lo:lo + n, :]
        elif s == hop + 1:
            for way in range(2):
                sum_copy(u, way, hop).wait_recv()
            rows = piece_rows(z, 0, piece)
            total = h_v[u, rows, :] + rs_v[u, 0, hop - 1] + rs_v[u, 1, hop - 1] + lanes(bcol1[rows, :], ch)
            g_v[u, pl.ds(pl.multiple_of(c * half_rows + z * piece, piece), piece), :] = gelu_of_half(0.5 * total).astype(BF16)
        else:
            for way in range(2):
                gather_copy(u, way, s - hop - 1, 1).wait_recv()

    def send_stage(u, s):
        if s <= hop:
            for way in range(2):
                launch(u, sum_copy(u, way, s))
        elif s <= 2 * hop:
            for way in range(2):
                launch(u, gather_copy(u, way, s - hop, 0))
        else:
            launch(u, share_copy(u, c))

    last_stage = 2 * hop + 2

    def store_out(u):
        return pltpu.make_async_copy(o_v.at[lax.rem(u, 2)], out_hbm.at[u], o_sem.at[lax.rem(u, 2)])

    def mix(u):
        share_copy(u, 1 - c).wait_recv()

        @pl.when(u >= 2)
        def _():
            store_out(u).wait()
        token_out_and_channel_mix(x_v.at[u], g_v.at[u], wt2t, bcol2, ln2s, ln2b, w1, b1h, w2, b2,
                                  x1_s, v_s, q_s, o_v.at[lax.rem(u, 2)])
        store_out(u).start()

    bcol1[...] = column(bt1[...])
    bcol2[...] = column(bt2[:, pl.ds(first, seq)])
    b1h[...] = 0.5 * b1[...]
    loads[0].wait()
    wt1t[...] = wt1_v[...].astype(F32).T.astype(BF16)
    project(0)
    pl.semaphore_wait(barrier, 3)
    pair_copy(0).start()
    project(1)
    pair_copy(1).start()
    loads[1].wait()
    wt2t[...] = wt2_v[...].astype(F32).T.astype(BF16)
    loads[2].wait()
    for r in range(0, ch, 128):
        w1[r:r + 128, :] = (w1[r:r + 128, :].astype(F32) * 0.5).astype(BF16)
    loads[3].wait()

    def tick(t, carry):
        for s in range(1, last_stage):
            u = t - s

            @pl.when(jnp.logical_and(u >= 0, u < units))
            def _(u=u, s=s):
                add_stage(u, s)
        for s in range(1, last_stage):
            u = t - s

            @pl.when(jnp.logical_and(u >= 0, u < units))
            def _(u=u, s=s):
                send_stage(u, s)

        @pl.when(2 * t < units)
        def _():
            for i in range(2):
                u = 2 * t + i
                project(u)
                launch(u, pair_copy(u))

        @pl.when(t >= last_stage)
        def _():
            mix(t - last_stage)
        return carry

    lax.fori_loop(1, units + last_stage, tick, 0)

    for u in (units - 2, units - 1):
        store_out(u).wait()
        pair_copy(u).wait_send()
        share_copy(u, c).wait_send()
        for way in range(2):
            for k in range(1, hop + 1):
                sum_copy(u, way, k).wait_send()
                gather_copy(u, way, k, 0).wait_send()


def fused_layer(nz, patches, ln1_scale, ln1_bias, w_tok1, b_tok1, w_tok2, b_tok2, ln2_scale, ln2_bias, w_ch1, b_ch1, w_ch2, b_ch2):
    units, seq, ch = patches.shape
    tok_hid = w_tok1.shape[1]
    hid = w_ch1.shape[1]
    hop = nz // 2
    piece = tok_hid // 2 // nz
    hbm = pl.BlockSpec(memory_space=pltpu.HBM)
    vmem = pl.BlockSpec(memory_space=pltpu.VMEM)
    row = lambda a: a.reshape(1, -1)
    return pl.pallas_call(
        functools.partial(fused_kernel, nz),
        out_shape=jax.ShapeDtypeStruct(patches.shape, BF16),
        in_specs=[hbm, vmem, vmem, hbm, vmem, hbm, vmem, vmem, vmem, hbm, vmem, hbm, vmem],
        out_specs=hbm,
        scratch_shapes=[
            pltpu.VMEM((units, seq, ch), BF16),
            pltpu.VMEM((units, tok_hid, ch), F32),
            pltpu.VMEM((units, tok_hid // 2, ch), F32),
            pltpu.VMEM((units, 2, hop, piece, ch), F32),
            pltpu.VMEM((units, tok_hid, ch), BF16),
            pltpu.VMEM((seq, tok_hid), BF16),
            pltpu.VMEM((tok_hid, seq), BF16),
            pltpu.VMEM((tok_hid, seq), BF16),
            pltpu.VMEM((seq, tok_hid), BF16),
            pltpu.VMEM((tok_hid, 128), F32),
            pltpu.VMEM((seq, 128), F32),
            pltpu.VMEM((ch, hid), BF16),
            pltpu.VMEM((hid, ch), BF16),
            pltpu.VMEM((1, hid), F32),
            pltpu.VMEM((seq, ch), BF16),
            pltpu.VMEM((seq, ch), BF16),
            pltpu.VMEM((seq, ch), BF16),
            pltpu.VMEM((seq, hid), BF16),
            pltpu.VMEM((2, seq, ch), BF16),
            pltpu.SemaphoreType.DMA((units,)),
            pltpu.SemaphoreType.DMA((4,)),
            pltpu.SemaphoreType.DMA((2,)),
            pltpu.SemaphoreType.DMA((2 + 4 * hop, 2)),
            pltpu.SemaphoreType.DMA((units,)),
            pltpu.SemaphoreType.DMA((units, 2, hop)),
            pltpu.SemaphoreType.DMA((units, 2, hop)),
            pltpu.SemaphoreType.DMA((units,)),
        ],
        compiler_params=pltpu.CompilerParams(collective_id=0, has_side_effects=True, vmem_limit_bytes=VMEM_LIMIT),
    )(patches, row(ln1_scale), row(ln1_bias), w_tok1, row(b_tok1), w_tok2, row(b_tok2),
      row(ln2_scale), row(ln2_bias), w_ch1, row(b_ch1), w_ch2, row(b_ch2))


def solution(mesh):
    row_spec = P('dp', 'sp', None)
    full_spec = P()
    nz = mesh.shape['sp'] // 2
    return jax.shard_map(functools.partial(fused_layer, nz), mesh=mesh, in_specs=(row_spec,) + (full_spec,) * 12,
                         out_specs=row_spec, check_vma=False)
```

time: 720 us -> 144 us (0.20)
  blocking collectives: 386 us -> 0 us
  local copies, waits for them, and re-layouts: 214 us -> 7.52 us
  Pallas kernels: 0 us -> 135 us
  matrix products: 72.8 us -> 0 us
  other arithmetic: 39.8 us -> 0 us
    all_to_all x2 -> x0, blocking collectives: 386 us -> none  [the longest x1 196 us: local_layer(): normed_cols = lax.all_to_all(normed, 'sp', 2, 1, tiled=True)]
    pallas_call x0 -> x1, Pallas kernels: none -> 135 us  [fused_layer(): pl.pallas_call(functools.partial(fused_kernel, nz), out_shape=jax.ShapeDt...]
    convert_element_type x4 -> x0, local copies, waits for them, and re-layouts: 78.8 us -> none  [the longest x1 34.6 us: local_layer(): mixed_cols = (mixed + b_tok2[None, :, None]).astype(jnp.bfloat16)]
    dot_general x4 -> x0, matrix products: 72.8 us -> none  [the longest x1 34 us: channel_mixing(): jnp.einsum('bsc,ce->bse', chan_in, w_ch1, preferred_element_type=jnp.floa...]
    unnamed x29 -> x1, local copies, waits for them, and re-layouts: 76.5 us -> 7.52 us
    all_to_all x3 -> x0, local copies, waits for them, and re-layouts: 58.7 us -> none  [the longest x1 33.7 us: local_layer(): mixed_rows = lax.all_to_all(mixed_cols, 'sp', 1, 2, tiled=True)]
    reduce_sum x4 -> x0, other arithmetic: 23.3 us -> none  [the longest x2 13.8 us: layer_norm(): row_mean = jnp.mean(rows_wide, axis=-1, keepdims=True)]
    convert_element_type x2 -> x0, other arithmetic: 16.5 us -> none  [the longest x1 11.3 us: local_layer(): mixed_rows.astype(jnp.float32)]
where the time goes in v1:
time: 144 us; the launch traced here: 143 us
  Pallas kernels  135 us (94%)
  local copies, waits for them, and re-layouts  7.52 us (5%)
    pallas_call x1, Pallas kernels, fused_layer(): pl.pallas_call(functools.partial(fused_kernel, nz), out_shape=jax.ShapeDt...  135 us
    unnamed x1, local copies, waits for them, and re-layouts  7.52 us

profile of v1, /device:TPU:21, one launch (start us, length us, event | category | flops | bytes accessed | tf_op | source)
XLA Modules:
  0.0 142.7 jit_solution(7511688600055252459)
XLA Ops:
  0.0 135.2 %shard_map.127 = bf16[16,512,512]{2,1,0:T(8,128)(2,1)} custom-call(bf16[16,512,512]{2,1,0:T(8,128)(2,1)} %x_hbm.1, f32[1,512]{1,0:T(1,128)} %bitcast.10, f32[1,512]{1,0:T(1,128)} %bitcast.11, bf16[8192,256]{1,0:T(8,128)(2,1)} %wt1_hbm.1, f32[1,256]{1,0:T(1,128)} %bitcast.15, bf16[256,8192]{1,0:T(8,128)(2,1)} %wt2_hbm.1, f32[1,8192]{1,0:T(1,128)} %bitcast.8, ...), custom_call_target="tpu_custom_call" | custom-call | tf_op jit(solution)/shard_map/pallas_call | solution.py:268
  135.2 7.5 %copy.15 = bf16[16,512,512]{2,1,0:T(8,128)(2,1)} copy(bf16[16,512,512]{2,1,0:T(8,128)(2,1)} %shard_map.127) | data formatting | bytes 16777216

commit v2 on v1

--- a/solution.py
+++ b/solution.py
@@ -12,6 +12,8 @@
 F32 = jnp.float32
 BF16 = jnp.bfloat16
 VMEM_LIMIT = 67043328
+PAIR_SLOTS = 2
+HOP_SLOTS = 3
 
 
 def layer_norm(wide, scale, offset):
@@ -42,10 +44,10 @@
     h_img[...] = jnp.dot(wt1t[...], u_s[...], preferred_element_type=F32)
 
 
-def token_out_and_channel_mix(x_img, g_img, wt2t, bcol2, ln2s, ln2b, w1, b1h, w2, b2, x1_s, v_s, q_s, o_img, rows=256, wide=512):
+def token_out_and_channel_mix(x_img, g_img, wt2t, bcol2, ln2s, ln2b, w1, b1h, w2, b2, x1_s, v_s, q_s, o_img, first=0, count=None, rows=256, wide=512):
     seq, ch = v_s.shape
     hid = w1.shape[1]
-    for r in range(0, seq, rows):
+    for r in range(first, first + (count or seq), rows):
         rs = slice(r, r + rows)
         mixed = jnp.dot(wt2t[rs, :], g_img[...], preferred_element_type=F32)
         mixed = (mixed + lanes(bcol2[rs, :], ch)).astype(BF16)
@@ -77,8 +79,12 @@
     mate = z * 2 + (1 - c)
     side = (right, left)
 
-    def at_z(offset):
-        return lax.rem(z + nz + offset, nz)
+    half_base = pl.multiple_of(c * half_rows, half_rows)
+    other_base = pl.multiple_of((1 - c) * half_rows, half_rows)
+    piece_base = [pl.multiple_of(c * half_rows + lax.rem(z + i, nz) * piece, piece) for i in range(nz)]
+
+    def base_at(distance):
+        return piece_base[distance % nz]
 
     barrier = pltpu.get_barrier_semaphore()
     for peer in (mate, right, left):
@@ -100,30 +106,27 @@
     for load in loads[1:]:
         load.start()
 
-    def remote(src, dst, slot, u, recv, peer):
+    def remote(src, dst, slot, recv, peer):
         return pltpu.make_async_remote_copy(
-            src_ref=src, dst_ref=dst, send_sem=send_sem.at[slot, lax.rem(u, 2)], recv_sem=recv,
+            src_ref=src, dst_ref=dst, send_sem=send_sem.at[slot], recv_sem=recv,
             device_id={'sp': peer}, device_id_type=pl.DeviceIdType.MESH)
 
     def pair_copy(u):
-        rows = pl.ds(pl.multiple_of((1 - c) * half_rows, half_rows), half_rows)
-        return remote(h_v.at[u, rows, :], d2d_v.at[u], 0, u, dr_sem.at[u], mate)
-
-    def piece_rows(home, lo, n):
-        return pl.ds(pl.multiple_of(c * half_rows + home * piece + lo, 8), n)
+        return remote(h_v.at[u, pl.ds(other_base, half_rows), :], d2d_v.at[u], 0, dr_sem.at[u], mate)
 
     def sum_part(way, k):
         if k > 1:
             return 0, piece
         return (0 if way == 0 else piece // 2), piece // 2
 
-    def sum_home(way, k):
-        return at_z(hop + 1 - k) if way == 0 else at_z(-(hop + 1 - k))
+    def sum_rows(way, k, lo, n):
+        base = base_at(hop + 1 - k if way == 0 else k - hop - 1)
+        return pl.ds(base if lo == 0 else pl.multiple_of(base + lo, 8), n)
 
     def sum_copy(u, way, k):
         lo, n = sum_part(way, k)
-        return remote(h_v.at[u, piece_rows(sum_home(way, k), lo, n), :], rs_v.at[u, way, k - 1, pl.ds(lo, n), :],
-                      1 + way * hop + k - 1, u, rr_sem.at[u, way, k - 1], side[way])
+        return remote(h_v.at[u, sum_rows(way, k, lo, n), :], rs_v.at[u, way, k - 1, pl.ds(lo, n), :],
+                      1 + way * hop + k - 1, rr_sem.at[u, way, k - 1], side[way])
 
     def gather_cols(way, k):
         if k < hop:
@@ -132,128 +135,127 @@
 
     def gather_copy(u, way, k, shift):
         d = k - 1 + shift
-        home = at_z(-d) if way == 0 else at_z(d)
-        rows = pl.ds(pl.multiple_of(c * half_rows + home * piece, piece), piece)
-        ref = g_v.at[u, rows, gather_cols(way, k)]
-        return remote(ref, ref, 1 + 2 * hop + way * hop + k - 1, u, ar_sem.at[u, way, k - 1], side[way])
-
-    def share_copy(u, core):
-        rows = pl.ds(pl.multiple_of(core * half_rows, half_rows), half_rows)
-        ref = g_v.at[u, rows, :]
-        return remote(ref, ref, 1 + 4 * hop, u, gr_sem.at[u], mate)
-
-    def launch(u, copy):
-        @pl.when(u >= 2)
-        def _():
-            copy.wait_send()
-        copy.start()
+        ref = g_v.at[u, pl.ds(base_at(-d if way == 0 else d), piece), gather_cols(way, k)]
+        return remote(ref, ref, 1 + 2 * hop + way * hop + k - 1, ar_sem.at[u, way, k - 1], side[way])
+
+    def share_copy(u, base):
+        ref = g_v.at[u, pl.ds(base, half_rows), :]
+        return remote(ref, ref, 1 + 4 * hop, gr_sem.at[u], mate)
+
+    def all_sent():
+        def sent(ref, slot):
+            remote(ref, ref, slot, dr_sem.at[0], mate).wait_send()
+        sent(d2d_v, 0)
+        sent(g_v.at[:, pl.ds(0, half_rows), :], 1 + 4 * hop)
+        for way in range(2):
+            for k in range(1, hop + 1):
+                lo, n = sum_part(way, k)
+                sent(rs_v.at[:, way, k - 1, pl.ds(lo, n), :], 1 + way * hop + k - 1)
+                sent(g_v.at[:, pl.ds(0, piece), gather_cols(way, k)], 1 + 2 * hop + way * hop + k - 1)
 
     def project(u):
         load_x(u).wait()
         norm_and_project(x_v.at[u], ln1s, ln1b, wt1t, u_s, h_v.at[u])
 
-    def own_rows():
-        return pl.ds(pl.multiple_of(c * half_rows, half_rows), half_rows)
-
-    def add_stage(u, s):
+    def serve_stage(u, s):
         if s == 1:
             pair_copy(u).wait_recv()
-            h_v[u, own_rows(), :] = h_v[u, own_rows(), :] + d2d_v[u]
+            rows = pl.ds(half_base, half_rows)
+            h_v[u, rows, :] = h_v[u, rows, :] + d2d_v[u]
         elif s <= hop:
             for way in range(2):
-                k = s - 1
-                sum_copy(u, way, k).wait_recv()
-                lo, n = sum_part(way, k)
-                rows = piece_rows(sum_home(way, s), lo, n)
-                h_v[u, rows, :] = h_v[u, rows, :] + rs_v[u, way, k - 1, lo:lo + n, :]
+                sum_copy(u, way, s - 1).wait_recv()
+            for way in range(2):
+                lo, n = sum_part(way, s - 1)
+                rows = sum_rows(way, s, lo, n)
+                h_v[u, rows, :] = h_v[u, rows, :] + rs_v[u, way, s - 2, lo:lo + n, :]
         elif s == hop + 1:
             for way in range(2):
                 sum_copy(u, way, hop).wait_recv()
-            rows = piece_rows(z, 0, piece)
+            rows = pl.ds(base_at(0), piece)
             total = h_v[u, rows, :] + rs_v[u, 0, hop - 1] + rs_v[u, 1, hop - 1] + lanes(bcol1[rows, :], ch)
-            g_v[u, pl.ds(pl.multiple_of(c * half_rows + z * piece, piece), piece), :] = gelu_of_half(0.5 * total).astype(BF16)
+            g_v[u, rows, :] = gelu_of_half(0.5 * total).astype(BF16)
         else:
             for way in range(2):
                 gather_copy(u, way, s - hop - 1, 1).wait_recv()
-
-    def send_stage(u, s):
         if s <= hop:
             for way in range(2):
-                launch(u, sum_copy(u, way, s))
+                sum_copy(u, way, s).start()
         elif s <= 2 * hop:
             for way in range(2):
-                launch(u, gather_copy(u, way, s - hop, 0))
+                gather_copy(u, way, s - hop, 0).start()
         else:
-            launch(u, share_copy(u, c))
+            share_copy(u, half_base).start()
 
     last_stage = 2 * hop + 2
+    delay = [0, PAIR_SLOTS]
+    for s in range(2, last_stage):
+        delay.append(delay[-1] + HOP_SLOTS)
+    fill = (delay[-1] + PAIR_SLOTS + 1) // 2
 
     def store_out(u):
         return pltpu.make_async_copy(o_v.at[lax.rem(u, 2)], out_hbm.at[u], o_sem.at[lax.rem(u, 2)])
 
-    def mix(u):
-        share_copy(u, 1 - c).wait_recv()
-
-        @pl.when(u >= 2)
-        def _():
-            store_out(u).wait()
+    def serve(t, p):
+        due = [(s, t - delay[s] // 2) for s in range(last_stage - 1, 0, -1) if delay[s] % 2 == p]
+        for s, u in due:
+            @pl.when(jnp.logical_and(u >= 0, u < units))
+            def _(u=u, s=s):
+                serve_stage(u, s)
+
+    def mix_half(u, p):
+        if p == 0:
+            share_copy(u, other_base).wait_recv()
+
+            @pl.when(u >= 2)
+            def _():
+                store_out(u).wait()
         token_out_and_channel_mix(x_v.at[u], g_v.at[u], wt2t, bcol2, ln2s, ln2b, w1, b1h, w2, b2,
-                                  x1_s, v_s, q_s, o_v.at[lax.rem(u, 2)])
-        store_out(u).start()
-
-    bcol1[...] = column(bt1[...])
-    bcol2[...] = column(bt2[:, pl.ds(first, seq)])
-    b1h[...] = 0.5 * b1[...]
+                                  x1_s, v_s, q_s, o_v.at[lax.rem(u, 2)], first=p * (seq // 2), count=seq // 2)
+        if p == 1:
+            store_out(u).start()
+
     loads[0].wait()
     wt1t[...] = wt1_v[...].astype(F32).T.astype(BF16)
     project(0)
     pl.semaphore_wait(barrier, 3)
     pair_copy(0).start()
-    project(1)
-    pair_copy(1).start()
-    loads[1].wait()
-    wt2t[...] = wt2_v[...].astype(F32).T.astype(BF16)
-    loads[2].wait()
-    for r in range(0, ch, 128):
-        w1[r:r + 128, :] = (w1[r:r + 128, :].astype(F32) * 0.5).astype(BF16)
-    loads[3].wait()
-
-    def tick(t, carry):
-        for s in range(1, last_stage):
-            u = t - s
-
-            @pl.when(jnp.logical_and(u >= 0, u < units))
-            def _(u=u, s=s):
-                add_stage(u, s)
-        for s in range(1, last_stage):
-            u = t - s
-
-            @pl.when(jnp.logical_and(u >= 0, u < units))
-            def _(u=u, s=s):
-                send_stage(u, s)
-
-        @pl.when(2 * t < units)
-        def _():
-            for i in range(2):
-                u = 2 * t + i
+    bcol1[...] = column(bt1[...])
+
+    def prepare_weights():
+        bcol2[...] = column(bt2[:, pl.ds(first, seq)])
+        b1h[...] = 0.5 * b1[...]
+        loads[1].wait()
+        wt2t[...] = wt2_v[...].astype(F32).T.astype(BF16)
+        loads[2].wait()
+        for r in range(0, ch, 128):
+            w1[r:r + 128, :] = (w1[r:r + 128, :].astype(F32) * 0.5).astype(BF16)
+        loads[3].wait()
+
+    def fill_tick(t, carry):
+        for p in range(2):
+            serve(t, p)
+            u = 2 * t + p
+
+            @pl.when(jnp.logical_and(u >= 1, u < units))
+            def _(u=u):
                 project(u)
-                launch(u, pair_copy(u))
-
-        @pl.when(t >= last_stage)
-        def _():
-            mix(t - last_stage)
+                pair_copy(u).start()
+        pl.when(t == units // 2)(prepare_weights)
         return carry
 
-    lax.fori_loop(1, units + last_stage, tick, 0)
+    def main_tick(t, carry):
+        for p in range(2):
+            serve(t, p)
+            mix_half(t - fill, p)
+        return carry
+
+    lax.fori_loop(0, fill, fill_tick, 0)
+    lax.fori_loop(fill, fill + units, main_tick, 0)
 
     for u in (units - 2, units - 1):
         store_out(u).wait()
-        pair_copy(u).wait_send()
-        share_copy(u, c).wait_send()
-        for way in range(2):
-            for k in range(1, hop + 1):
-                sum_copy(u, way, k).wait_send()
-                gather_copy(u, way, k, 0).wait_send()
+    all_sent()
 
 
 def fused_layer(nz, patches, ln1_scale, ln1_bias, w_tok1, b_tok1, w_tok2, b_tok2, ln2_scale, ln2_bias, w_ch1, b_ch1, w_ch2, b_ch2):
@@ -293,7 +295,7 @@
             pltpu.SemaphoreType.DMA((units,)),
             pltpu.SemaphoreType.DMA((4,)),
             pltpu.SemaphoreType.DMA((2,)),
-            pltpu.SemaphoreType.DMA((2 + 4 * hop, 2)),
+            pltpu.SemaphoreType.DMA((2 + 4 * hop,)),
             pltpu.SemaphoreType.DMA((units,)),
             pltpu.SemaphoreType.DMA((units, 2, hop)),
             pltpu.SemaphoreType.DMA((units, 2, hop)),

time: 144 us -> 125 us (0.87)
  Pallas kernels: 135 us -> 116 us
    pallas_call x1, Pallas kernels: 135 us -> 116 us  [fused_layer(): pl.pallas_call(functools.partial(fused_kernel, nz), out_shape=jax.ShapeDt...]
where the time goes in v2:
time: 125 us; the launch traced here: 123 us
  Pallas kernels  116 us (93%)
  local copies, waits for them, and re-layouts  7.52 us (6%)
    pallas_call x1, Pallas kernels, fused_layer(): pl.pallas_call(functools.partial(fused_kernel, nz), out_shape=jax.ShapeDt...  116 us
    unnamed x1, local copies, waits for them, and re-layouts  7.52 us

profile of v2, /device:TPU:21, one launch (start us, length us, event | category | flops | bytes accessed | tf_op | source)
XLA Modules:
  0.0 123.4 jit_solution(14439430322472107298)
XLA Ops:
  0.0 115.8 %shard_map.127 = bf16[16,512,512]{2,1,0:T(8,128)(2,1)} custom-call(bf16[16,512,512]{2,1,0:T(8,128)(2,1)} %x_hbm.1, f32[1,512]{1,0:T(1,128)} %bitcast.10, f32[1,512]{1,0:T(1,128)} %bitcast.11, bf16[8192,256]{1,0:T(8,128)(2,1)} %wt1_hbm.1, f32[1,256]{1,0:T(1,128)} %bitcast.15, bf16[256,8192]{1,0:T(8,128)(2,1)} %wt2_hbm.1, f32[1,8192]{1,0:T(1,128)} %bitcast.8, ...), custom_call_target="tpu_custom_call" | custom-call | tf_op jit(solution)/shard_map/pallas_call | solution.py:270
  115.8 7.5 %copy.15 = bf16[16,512,512]{2,1,0:T(8,128)(2,1)} copy(bf16[16,512,512]{2,1,0:T(8,128)(2,1)} %shard_map.127) | data formatting | bytes 16777216
